TPU v7x, 32 devices: a whole 2x2x4 slice. The times are simulated.
32 devices in a mesh: rows: 8 (over y, x, core), feat: 4 (over z).
Axes of the slice: x: 2, y: 2, z: 4, core: 2. Of those that a mesh axis runs over, the one named last changes fastest.
Arguments:
- features: bfloat16 [8192, 2048], P('rows', 'feat'), may hold values from -6 to 6
- grad_out: bfloat16 [8192, 2048], P('rows', 'feat'), may hold values from -6 to 6
- eigvecs: float32 [2048, 2048], P('feat', 'rows'), may hold values from -1 to 1, as said below
- eigvals: float32 [2048], replicated, may hold values from 0.1 to 1, as said below
- whiten: bfloat16 [2048, 2048], P(None, 'feat'), may hold values from -0.125 to 0.125
Outputs:
- grad_in: bfloat16 [8192, 2048], P('rows', 'feat')
Inputs may be any that keep to these rules, and one draw needn't show every extreme that they name: `eigvecs`: the columns are orthonormal. `eigvals`: any two entries differ by at least 0.45 / 2048.
All inputs are finite; a program needn't handle non-finite values.
Results may differ from a plain program's by a relative error of at most 0.0074.
Values may be sent and summed in bfloat16 or wider, within the bound.
A program may use at most 128 MiB of HBM per device.

v0:
```python
import jax
import jax.numpy as jnp
from jax import lax
from jax.sharding import PartitionSpec as P


def divided(lam_row, lam_col, first_col):
    on_diag = (
        jnp.arange(lam_row.shape[0], dtype=jnp.int32)[:, None]
        == (first_col + jnp.arange(lam_col.shape[0], dtype=jnp.int32))[None, :]
    )
    root_row = lam_row ** (-0.5)
    root_col = lam_col ** (-0.5)
    gaps_lam = lam_row[:, None] - lam_col[None, :]
    safe_gap = jnp.where(on_diag, jnp.ones_like(gaps_lam), gaps_lam)
    off_diag = (root_row[:, None] - root_col[None, :]) / safe_gap
    diag_vals = -0.5 * lam_row[:, None] ** (-1.5) + jnp.zeros_like(gaps_lam)
    return jnp.where(on_diag, diag_vals, off_diag)


def local(features, grad_out, eigvecs, eigvals, whiten):
    highest = lax.Precision.HIGHEST
    tok_rows, own_cols = features.shape
    row_count = tok_rows * lax.axis_size("rows")
    contract_rows = (((0,), (0,)), ((), ()))
    contract_last = (((1,), (1,)), ((), ()))
    piece_x = lax.all_gather(features, "feat", axis=1, tiled=True)
    piece_g = lax.all_gather(grad_out, "feat", axis=1, tiled=True)
    left_part = lax.dot_general(
        features, piece_g, contract_rows, preferred_element_type=jnp.float32
    )
    right_part = lax.dot_general(
        grad_out, piece_x, contract_rows, preferred_element_type=jnp.float32
    )
    cross_one = left_part
    cross_two = right_part
    sum_x = jnp.sum(piece_x, axis=0, dtype=jnp.float32)
    sum_g = jnp.sum(piece_g, axis=0, dtype=jnp.float32)
    cross_one, cross_two, sum_x, sum_g = (cross_one, cross_two, sum_x, sum_g)
    cross_one, cross_two, sum_x, sum_g = lax.psum((cross_one, cross_two, sum_x, sum_g), "rows")
    both_cross = cross_one + cross_two
    col_mean = sum_x / row_count
    grad_mean = sum_g / row_count
    offset = lax.axis_index("feat") * own_cols
    mean_part = lax.dynamic_slice_in_dim(col_mean, offset, own_cols)
    grad_part = lax.dynamic_slice_in_dim(grad_mean, offset, own_cols)
    sym_gram = 0.5 * (
        both_cross
        - row_count
        * (mean_part[:, None] * grad_mean[None, :] + grad_part[:, None] * col_mean[None, :])
    )
    basis_cols = lax.all_gather(eigvecs, "feat", axis=0, tiled=True)
    basis_block = lax.all_gather(eigvecs, "rows", axis=1, tiled=True)
    narrow = basis_cols.shape[1]
    inner_prod = jnp.dot(sym_gram, basis_cols, precision=highest)
    partial_value = lax.dot_general(basis_block, inner_prod, contract_rows, precision=highest)
    rotated = lax.psum(partial_value, "feat")
    first_col = lax.axis_index("rows") * narrow
    lam_col = lax.dynamic_slice_in_dim(eigvals, first_col, narrow)
    scaled = divided(eigvals, lam_col, first_col) * rotated
    back_rot = jnp.dot(basis_block, scaled, precision=highest)
    sens_own = lax.psum_scatter(
        lax.dot_general(back_rot, basis_cols, contract_last, precision=highest),
        "rows",
        scatter_dimension=0,
        tiled=True,
    )
    scaled_own = (2.0 / row_count * sens_own).astype(jnp.bfloat16)
    sens_scaled = lax.all_gather(scaled_own, "rows", axis=0, tiled=True)
    piece_x = lax.all_gather(features, "feat", axis=1, tiled=True)
    piece_g = lax.all_gather(grad_out, "feat", axis=1, tiled=True)
    shifted = (piece_g.astype(jnp.float32) - grad_mean).astype(jnp.bfloat16)
    centered = (piece_x.astype(jnp.float32) - col_mean).astype(jnp.bfloat16)
    running = jnp.dot(shifted, whiten, preferred_element_type=jnp.float32)
    grad_in = running + lax.dot_general(
        centered, sens_scaled, contract_last, preferred_element_type=jnp.float32
    )
    return grad_in.astype(jnp.bfloat16)


def solution(mesh):
    in_specs = (P("rows", "feat"), P("rows", "feat"), P("feat", "rows"), P(), P(None, "feat"))
    out_specs = P("rows", "feat")
    return jax.shard_map(local, mesh=mesh, in_specs=in_specs, out_specs=out_specs, check_vma=False)
```

profile of v0, /device:TPU:25, one launch (start us, length us, event | category | flops | bytes accessed | tf_op | source)
XLA Modules:
  0.0 550.9 jit_solution(13871746332786428748)
XLA Ops:
  6.5 0.7 all-gather.6.cloned.1.call-update
  7.3 0.7 all-gather.8.cloned.1.call-update
  8.1 0.7 all-gather.10.cloned.1.call-update
  8.8 79.3 %all-gather.6.cloned.1.call-done = bf16[1024,2048]{1,0:T(8,128)(2,1)} async-done(((bf16[1024,512]{1,0:T(8,128)(2,1)}), bf16[1024,2048]{1,0:T(8,128)(2,1)}) %all-gather.6.cloned.1.call-update) | async-done | bytes 4194320 | tf_op jit(solution)/shard_map/all_gather | solution.py:71
  88.1 6.8 %fusion.40 = f32[512,2048]{1,0:T(8,128)} fusion(bf16[1024,512]{1,0:T(8,128)(2,1)} %param.5, bf16[1024,2048]{1,0:T(8,128)(2,1)} %all-gather.6.cloned.1.call-done), kind=kOutput, calls=%fused_computation.51 | convolution fusion | flops 2147483648 | bytes 9437184 | tf_op jit(solution)/shard_map/dot_general | solution.py:29
  94.9 74.0 %all-gather.8.cloned.1.call-done = bf16[1024,2048]{1,0:T(8,128)(2,1)} async-done(((bf16[1024,512]{1,0:T(8,128)(2,1)}), bf16[1024,2048]{1,0:T(8,128)(2,1)}) %all-gather.8.cloned.1.call-update) | async-done | bytes 4194320 | tf_op jit(solution)/shard_map/all_gather | solution.py:70
  168.9 7.8 %convolution_add_fusion = f32[512,2048]{1,0:T(8,128)} fusion(f32[512,2048]{1,0:T(8,128)} %fusion.40, bf16[1024,512]{1,0:T(8,128)(2,1)S(1)} %copy-done.3, bf16[1024,2048]{1,0:T(8,128)(2,1)} %all-gather.8.cloned.1.call-done), kind=kOutput, calls=%fused_computation.17 | convolution fusion | flops 2148532224 | bytes 13631488 | tf_op jit(solution)/shard_map/dot_general | solution.py:32
  177.4 3.2 convert_reduce_fusion
  180.6 0.6 copy-done.1
  181.3 0.6 convert_reduce_fusion.1
  181.9 22.9 %all-reduce = (f32[2048]{0:T(1024)S(1)}, f32[2048]{0:T(1024)S(1)}) all-reduce(f32[2048]{0:T(1024)S(1)} %convert_reduce_fusion, f32[2048]{0:T(1024)S(1)} %convert_reduce_fusion.1), channel_id=1, replica_groups=mesh['rows'=8,'feat'=4] {'rows'}, use_global_device_ids=true, to_apply=%region_3.0 | all-reduce | flops 4096 | bytes 32768 | tf_op jit(solution)/shard_map/psum | solution.py:40
  205.0 10.5 %all-gather.10.cloned.1.call-done = f32[2048,256]{1,0:T(8,128)} async-done(((f32[512,256]{1,0:T(8,128)}), f32[2048,256]{1,0:T(8,128)}) %all-gather.10.cloned.1.call-update) | async-done | bytes 2097168 | tf_op jit(solution)/shard_map/all_gather | solution.py:52
  215.5 84.3 %all-reduce.6.cloned.1.call-done = f32[512,2048]{1,0:T(8,128)} async-done(((f32[512,2048]{1,0:T(8,128)}), f32[512,2048]{1,0:T(8,128)}) %all-reduce.6.cloned.1.call-update) | async-done | bytes 4194320 | tf_op jit(solution)/shard_map/psum | solution.py:40
  299.8 6.9 %fusion.6 = f32[512,256]{1,0:T(8,128)S(1)} fusion(f32[2048,256]{1,0:T(8,128)} %all-gather.10.cloned.1.call-done, f32[512,2048]{1,0:T(8,128)} %all-reduce.6.cloned.1.call-done, f32[2048]{0:T(1024)S(1)} %get-tuple-element.11, f32[512]{0:T(512)S(1)} %dynamic_slice.11, f32[2048]{0:T(1024)S(1)} %get-tuple-element.12, f32[512]{0:T(512)S(1)} %dynamic_slice.10), kind=kOutput, calls=%fused_computation.8 | convolution fusion | flops 3227516928 | bytes 6836224 | tf_op jit(solution)/shard_map/dot_general | solution.py:55
  306.7 32.9 %all-gather.12.cloned.1.call-done = f32[512,2048]{1,0:T(8,128)} async-done(((f32[512,256]{1,0:T(8,128)}), f32[512,2048]{1,0:T(8,128)}) %all-gather.12.cloned.1.call-update) | async-done | bytes 4194320 | tf_op jit(solution)/shard_map/all_gather | solution.py:53
  339.6 10.2 %convolution_bitcast_fusion = f32[2048,256]{1,0:T(8,128)} fusion(f32[512,256]{1,0:T(8,128)S(1)} %fusion.6, f32[512,2048]{1,0:T(8,128)} %all-gather.12.cloned.1.call-done), kind=kOutput, calls=%fused_computation.18 | convolution fusion | flops 3221225472 | bytes 6815744 | tf_op jit(solution)/shard_map/dot_general | solution.py:56
  350.2 83.9 %all-reduce.4.cloned.1.call-done = f32[2048,256]{1,0:T(8,128)} async-done(((f32[2048,256]{1,0:T(8,128)}), f32[2048,256]{1,0:T(8,128)}) %all-reduce.4.cloned.1.call-update) | async-done | bytes 2097168 | tf_op jit(solution)/shard_map/psum | solution.py:57
  434.1 10.8 %fusion.15 = f32[256,512]{1,0:T(8,128)S(1)} fusion(f32[512,2048]{1,0:T(8,128)} %all-gather.12.cloned.1.call-done, f32[2048,256]{1,0:T(8,128)} %all-reduce.4.cloned.1.call-done, f32[256]{0:T(256)S(1)} %get-tuple-element.8, f32[2048]{0:T(1024)S(1)} %copy-done.5, f32[256]{0:T(256)S(1)} %get-tuple-element.7, f32[2048]{0:T(1024)S(1)} %get-tuple-element.10, ...), kind=kOutput, calls=%fused_computation.20 | convolution fusion | flops 3224895488 | bytes 6843392 | tf_op jit(solution)/shard_map/dot_general | solution.py:61
  444.9 8.4 %fusion.41 = f32[512,2048]{1,0:T(8,128)} fusion(f32[256,512]{1,0:T(8,128)S(1)} %fusion.15, f32[2048,256]{1,0:T(8,128)S(1)} %copy-done.4), kind=kOutput, calls=%fused_computation.52 | convolution fusion | flops 3221225472 | bytes 6815744 | tf_op jit(solution)/shard_map/dot_general | solution.py:63
  453.7 51.4 %reduce-scatter.2.cloned.1.call-done = f32[64,2048]{1,0:T(8,128)} async-done(((f32[512,2048]{1,0:T(8,128)}), f32[64,2048]{1,0:T(8,128)}) %reduce-scatter.2.cloned.1.call-update) | async-done | bytes 524304 | tf_op jit(solution)/shard_map/reduce_scatter | solution.py:62
  505.1 1.8 multiply_convert_fusion
  506.9 28.5 %all-gather.14.cloned.1.call-done = bf16[512,2048]{1,0:T(8,128)(2,1)} async-done(((bf16[64,2048]{1,0:T(8,128)(2,1)}), bf16[512,2048]{1,0:T(8,128)(2,1)}) %all-gather.14.cloned.1.call-update) | async-done | bytes 2097168 | tf_op jit(solution)/shard_map/all_gather | solution.py:69
  535.4 5.4 fusion.2
  540.8 3.3 add_convert_fusion
  (30 shorter events, 1.6 us)
Async XLA Ops:
  6.5 534.2 %copy-start = (bf16[2048,512]{1,0:T(8,128)(2,1)S(1)}, bf16[2048,512]{1,0:T(8,128)(2,1)}, u32[]{:S(2)}) copy-start(bf16[2048,512]{1,0:T(8,128)(2,1)} %param.9) | copy-start | bytes 6291460
  6.5 81.5 %all-gather.6.cloned.1.call-start = ((), (), s32[]{:S(2)}) async-start(), calls=%async_computation.1 | async-start | bytes 5242880 | tf_op jit(solution)/shard_map/all_gather | solution.py:71
  7.3 161.6 %all-gather.8.cloned.1.call-start = ((), (), s32[]{:S(2)}) async-start(), calls=%async_computation.2 | async-start | bytes 5242880 | tf_op jit(solution)/shard_map/all_gather | solution.py:70
  8.0 207.5 %all-gather.10.cloned.1.call-start = ((), (), s32[]{:S(2)}) async-start(), calls=%async_computation.3 | async-start | bytes 2621440 | tf_op jit(solution)/shard_map/all_gather | solution.py:52
  8.7 160.2 %copy-start.3 = (bf16[1024,512]{1,0:T(8,128)(2,1)S(1)}, bf16[1024,512]{1,0:T(8,128)(2,1)}, u32[]{:S(2)}) copy-start(bf16[1024,512]{1,0:T(8,128)(2,1)} %param.6) | copy-start | bytes 3145732
  8.8 291.0 %all-reduce.6.cloned.1.call-start = ((), (), s32[]{:S(2)}) async-start(), calls=%async_computation.8 | async-start | bytes 8388608 | tf_op jit(solution)/shard_map/psum | solution.py:40
  176.7 162.8 %all-gather.12.cloned.1.call-start = ((), (), s32[]{:S(2)}) async-start(), calls=%async_computation.4 | async-start | bytes 4718592 | tf_op jit(solution)/shard_map/all_gather | solution.py:53
  177.3 256.8 %all-reduce.4.cloned.1.call-start = ((), (), s32[]{:S(2)}) async-start(), calls=%async_computation.5 | async-start | bytes 4194304 | tf_op jit(solution)/shard_map/psum | solution.py:57
  177.4 3.9 copy-start.1
  306.6 43.4 %copy-start.5 = (f32[2048]{0:T(1024)S(1)}, f32[2048]{0:T(1024)}, u32[]{:S(2)}) copy-start(f32[2048]{0:T(1024)} %param.8) | copy-start | bytes 24580
  349.8 155.3 %reduce-scatter.2.cloned.1.call-start = ((), (), s32[]{:S(2)}) async-start(), calls=%async_computation.6 | async-start | bytes 4718592 | tf_op jit(solution)/shard_map/reduce_scatter | solution.py:62
  434.1 10.8 %copy-start.4 = (f32[2048,256]{1,0:T(8,128)S(1)}, f32[2048,256]{1,0:T(8,128)}, u32[]{:S(2)}) copy-start(f32[2048,256]{1,0:T(8,128)} %all-gather.10.cloned.1.call-done) | copy-start | bytes 6291460
  453.4 82.0 %all-gather.14.cloned.1.call-start = ((), (), s32[]{:S(2)}) async-start(), calls=%async_computation.7 | async-start | bytes 2359296 | tf_op jit(solution)/shard_map/all_gather | solution.py:69
  535.4 5.4 copy-start.2
Sparse Core Ops, SparseCore 0:
  8.9 79.1 all-gather.5
  89.6 79.2 all-gather.7
  170.5 44.9 all-gather.9
  218.6 81.1 all-reduce.5
  301.5 38.0 all-gather.11
  349.9 84.1 all-reduce.3
  453.5 51.5 reduce-scatter.1
  507.0 28.3 all-gather.13
where the time goes:
time: 552 us; the launch traced here: 551 us
  waiting for transfers between devices  448 us (81%)
  matrix products  59.6 us (11%)
  blocking collectives  22.9 us (4%)
  between operations  13.6 us (2%)
  other arithmetic  5.64 us (1%)
    psum x1, waiting for transfers between devices, local(): lax.psum((cross_one, cross_two, sum_x, sum_g), 'rows')  84.3 us
    psum x1, waiting for transfers between devices, local(): rotated = lax.psum(partial_value, 'feat')  83.9 us
    all_gather x1, waiting for transfers between devices, local(): piece_g = lax.all_gather(grad_out, 'feat', axis=1, tiled=True)  79.3 us
    all_gather x1, waiting for transfers between devices, local(): piece_x = lax.all_gather(features, 'feat', axis=1, tiled=True)  74 us
    reduce_scatter x1, waiting for transfers between devices, local(): lax.psum_scatter(lax.dot_general(back_rot, basis_cols, contract_last, pre...  51.4 us
    all_gather x1, waiting for transfers between devices, local(): basis_block = lax.all_gather(eigvecs, 'rows', axis=1, tiled=True)  32.9 us
    all_gather x1, waiting for transfers between devices, local(): sens_scaled = lax.all_gather(scaled_own, 'rows', axis=0, tiled=True)  28.5 us
    psum x1, blocking collectives, local(): lax.psum((cross_one, cross_two, sum_x, sum_g), 'rows')  22.9 us
  transfers between devices with their start and end apart: 8, of which 8 were waited for; matrix products, arithmetic and copies ran while one was open for 5% of the time, Pallas kernels for 0%

commit v1 on v0

v1 whole, which is shorter than its diff:
```python
import functools

import jax
import jax.numpy as jnp
from jax import lax
from jax.experimental import pallas as pl
from jax.experimental.pallas import tpu as pltpu
from jax.sharding import PartitionSpec as P

MESH = pl.DeviceIdType.MESH
VMEM = pl.BlockSpec(memory_space=pltpu.VMEM)
bf16, f32 = jnp.bfloat16, jnp.float32


def peer(axis, index):
    return {axis: index}


def greet(axis, targets):
    barrier = pltpu.get_barrier_semaphore()
    for target in targets:
        pl.semaphore_signal(barrier, inc=1, device_id=peer(axis, target), device_id_type=MESH)
    pl.semaphore_wait(barrier, len(targets))


def remote(src, dst, send, recv, axis, target):
    return pltpu.make_async_remote_copy(
        src_ref=src, dst_ref=dst, send_sem=send, recv_sem=recv,
        device_id=peer(axis, target), device_id_type=MESH,
    )


def exchange_kernel(axis, n, same, x_ref, o_ref, send, recv):
    me = lax.axis_index(axis)
    targets = [lax.rem(me + d, n) for d in range(1, n)]
    greet(axis, targets)
    copies = []
    for d in range(1, n):
        src = x_ref if same else x_ref.at[targets[d - 1]]
        copy = remote(src, o_ref.at[me], send.at[d - 1], recv.at[d - 1], axis, targets[d - 1])
        copy.start()
        copies.append(copy)
    o_ref[me] = x_ref[...] if same else x_ref[me]
    for copy in copies:
        copy.wait()


def gather_kernel(axis, n, x_ref, o_ref, send, recv, core_send, core_recv):
    me = lax.axis_index(axis)
    core = lax.rem(me, 2)
    mate = me + 1 - 2 * core
    h = n // 2
    targets = [lax.rem(me + 2 * d, n) for d in range(1, h)]
    greet(axis, [mate] + targets)
    copies = []
    for d in range(1, h):
        copy = remote(x_ref, o_ref.at[me], send.at[d], recv.at[d], axis, targets[d - 1])
        copy.start()
        copies.append(copy)
    passed = [remote(x_ref, o_ref.at[me], core_send.at[0], core_recv.at[0], axis, mate)]
    passed[0].start()
    o_ref[me] = x_ref[...]
    for d in range(1, h):
        source = lax.rem(me + n - 2 * d, n)
        copies[d - 1].wait_recv()
        copy = remote(o_ref.at[source], o_ref.at[source], core_send.at[d], core_recv.at[d], axis, mate)
        copy.start()
        passed.append(copy)
    for copy in copies:
        copy.wait_send()
    for copy in passed:
        copy.wait()


def scatter_kernel(axis, n, x_ref, o_ref, landed, stage, parts, send, recv, core_send, core_recv):
    me = lax.axis_index(axis)
    core = lax.rem(me, 2)
    chip = me // 2
    mate = me + 1 - 2 * core
    h = n // 2
    targets = [lax.rem(me + 2 * d, n) for d in range(1, h)]
    greet(axis, [mate] + targets)
    core_copies = []
    for d in list(range(1, h)) + [0]:
        there = lax.rem(chip + d, h)
        copy = remote(x_ref.at[1 - core, there], landed.at[d], core_send.at[d], core_recv.at[d], axis, mate)
        copy.start()
        core_copies.append(copy)
    copies = []
    for order, d in enumerate(range(1, h)):
        there = lax.rem(chip + d, h)
        core_copies[order].wait_recv()
        stage[d - 1] = (x_ref[core, there].astype(f32) + landed[d].astype(f32)).astype(bf16)
        copy = remote(stage.at[d - 1], parts.at[d - 1], send.at[d - 1], recv.at[d - 1], axis, targets[d - 1])
        copy.start()
        copies.append(copy)
    core_copies[-1].wait_recv()
    total = x_ref[core, chip].astype(f32) + landed[0].astype(f32)
    for d in range(1, h):
        copies[d - 1].wait_recv()
        total = total + parts[d - 1].astype(f32)
    o_ref[...] = total.astype(bf16)
    for copy in copies + core_copies:
        copy.wait_send()


def call(kernel, out, scratch, cid, sent, *args):
    return pl.pallas_call(
        kernel,
        out_shape=out,
        in_specs=[VMEM] * len(args),
        out_specs=VMEM,
        scratch_shapes=scratch,
        compiler_params=pltpu.CompilerParams(collective_id=cid, has_side_effects=True, vmem_limit_bytes=48 * 2**20),
        cost_estimate=pl.CostEstimate(flops=8_000_000_000, bytes_accessed=sent, transcendentals=0),
    )(*args)


def exchange(x, axis, cid, same=False):
    n = lax.axis_size(axis)
    shape = (n,) + x.shape if same else x.shape
    sems = [pltpu.SemaphoreType.DMA((n - 1,))] * 2
    return call(functools.partial(exchange_kernel, axis, n, same), jax.ShapeDtypeStruct(shape, x.dtype), sems, cid, x.nbytes, x)


def gather(x, axis, cid):
    n = lax.axis_size(axis)
    sems = [pltpu.SemaphoreType.DMA((n // 2,))] * 4
    return call(functools.partial(gather_kernel, axis, n), jax.ShapeDtypeStruct((n,) + x.shape, x.dtype), sems, cid, x.nbytes, x)


def scatter(x, axis, cid):
    n = lax.axis_size(axis)
    h, piece = n // 2, x.shape[2:]
    scratch = [pltpu.VMEM((h,) + piece, bf16), pltpu.VMEM((h,) + piece, bf16), pltpu.VMEM((h,) + piece, bf16)]
    scratch += [pltpu.SemaphoreType.DMA((h,))] * 4
    return call(functools.partial(scatter_kernel, axis, n), jax.ShapeDtypeStruct(piece, bf16), scratch, cid, x.nbytes, x)


def divided(lam_row, lam_col, first_row):
    on_diag = (
        (first_row + jnp.arange(lam_row.shape[0], dtype=jnp.int32))[:, None]
        == jnp.arange(lam_col.shape[0], dtype=jnp.int32)[None, :]
    )
    root_row = lam_row ** (-0.5)
    root_col = lam_col ** (-0.5)
    gaps_lam = lam_row[:, None] - lam_col[None, :]
    safe_gap = jnp.where(on_diag, jnp.ones_like(gaps_lam), gaps_lam)
    off_diag = (root_row[:, None] - root_col[None, :]) / safe_gap
    diag_vals = -0.5 * lam_row[:, None] ** (-1.5) + jnp.zeros_like(gaps_lam)
    return jnp.where(on_diag, diag_vals, off_diag)


def dot(a, b, ca, cb):
    return lax.dot_general(a, b, (((ca,), (cb,)), ((), ())), preferred_element_type=f32)


def local(features, grad_out, eigvecs, eigvals, whiten):
    tok_rows, own = features.shape
    n = lax.axis_size("rows")
    d_all = eigvals.shape[0]
    nar = d_all // n
    row_count = tok_rows * n
    me = lax.axis_index("rows")

    v_col = lax.all_gather(eigvecs.astype(bf16), "feat", axis=0, tiled=True)
    sums = jnp.stack([jnp.sum(features, axis=0, dtype=f32), jnp.sum(grad_out, axis=0, dtype=f32)])
    sums = jnp.pad(sums, ((0, 6), (0, 0)))
    means = jnp.sum(gather(sums, "rows", 1), axis=0) / row_count
    xc = (features.astype(f32) - means[0]).astype(bf16)
    gc = (grad_out.astype(f32) - means[1]).astype(bf16)
    g_all = lax.all_gather(gc, "feat", axis=1, tiled=True)
    v_all = gather(v_col, "rows", 2).transpose(1, 0, 2).reshape(d_all, d_all)

    xc, g_all = lax.optimization_barrier((xc, g_all))
    x_all = lax.all_gather(xc, "feat", axis=1, tiled=True)
    part = dot(xc, g_all, 0, 0).astype(bf16)
    part = part.reshape(own, n // 2, 2, nar).transpose(2, 1, 0, 3)
    tile = scatter(part, "rows", 3)
    c_col = exchange(tile, "feat", 4, same=True).reshape(n, nar, nar)
    turned = exchange(c_col, "rows", 5)
    both = 0.5 * (c_col.astype(f32) + turned.transpose(0, 2, 1).astype(f32))
    both = both.reshape(d_all, nar).astype(bf16)
    half = dot(v_all, both, 0, 0).astype(bf16)
    half = exchange(half.reshape(n, nar, nar), "rows", 6)
    rotated = dot(half.transpose(1, 0, 2).reshape(nar, d_all), v_all, 1, 0)
    first = me * nar
    lam_row = lax.dynamic_slice_in_dim(eigvals, first, nar)
    scaled = (divided(lam_row, eigvals, first) * rotated).astype(bf16)
    back = dot(scaled, v_all, 1, 1).astype(bf16)
    back = exchange(back.reshape(nar, n, nar).transpose(1, 0, 2), "rows", 7).reshape(d_all, nar)
    v_own = lax.dynamic_slice_in_dim(v_all, lax.axis_index("feat") * own, own)
    sens = (2.0 / row_count * dot(v_own, back, 1, 0)).astype(bf16)
    sens = gather(sens, "rows", 8).transpose(1, 0, 2).reshape(own, d_all)
    grad_in = dot(g_all, whiten, 1, 0) + dot(x_all, sens, 1, 1)
    return grad_in.astype(bf16)


def solution(mesh):
    in_specs = (P("rows", "feat"), P("rows", "feat"), P("feat", "rows"), P(), P(None, "feat"))
    out_specs = P("rows", "feat")
    return jax.shard_map(local, mesh=mesh, in_specs=in_specs, out_specs=out_specs, check_vma=False)
```

time: 552 us -> 325 us (0.59)
  waiting for transfers between devices: 448 us -> 27.6 us
  Pallas kernels: 0 us -> 196 us
  local copies, waits for them, and re-layouts: 0.9 us -> 38.7 us
  blocking collectives: 22.9 us -> 0 us
  matrix products: 59.6 us -> 39.1 us
    all_gather x5 -> x3, waiting for transfers between devices: 225 us -> 27.6 us  [the longest x1 15.8 us: local(): v_col = lax.all_gather(eigvecs.astype(bf16), 'feat', axis=0, tiled=True)]
    pallas_call x0 -> x8, Pallas kernels: none -> 196 us  [call(): pl.pallas_call(kernel, out_shape=out, in_specs=[VMEM] * len(args), out_sp...]
    psum x2 -> x0, waiting for transfers between devices: 168 us -> none  [the longest x1 84.3 us: local(): lax.psum((cross_one, cross_two, sum_x, sum_g), 'rows')]
    reduce_scatter x1 -> x0, waiting for transfers between devices: 51.4 us -> none  [local(): lax.psum_scatter(lax.dot_general(back_rot, basis_cols, contract_last, pre...]
    psum x1 -> x0, blocking collectives: 22.9 us -> none  [local(): lax.psum((cross_one, cross_two, sum_x, sum_g), 'rows')]
    dot_general x8 -> x6, matrix products: 59.6 us -> 39.1 us  [dot(): lax.dot_general(a, b, (((ca,), (cb,)), ((), ())), preferred_element_type=...]
    transpose x0 -> x3, local copies, waits for them, and re-layouts: none -> 17 us  [the longest x1 11.6 us: local(): v_all = gather(v_col, 'rows', 2).transpose(1, 0, 2).reshape(d_all, d_all)]
    convert_element_type x0 -> x3, local copies, waits for them, and re-layouts: none -> 7.69 us  [the longest x1 3.91 us: local(): part = dot(xc, g_all, 0, 0).astype(bf16)]
  transfers between devices with their start and end apart: 8 -> 3, of which waited for: 8 -> 2; matrix products, arithmetic and copies ran while one was open for 5% -> 22% of each run, Pallas kernels for 0% -> 61%
where the time goes in v1:
time: 325 us; the launch traced here: 324 us
  Pallas kernels  196 us (60%)
  matrix products  39.1 us (12%)
  local copies, waits for them, and re-layouts  38.7 us (12%)
  waiting for transfers between devices  27.6 us (8%)
  between operations  13.3 us (4%)
  other arithmetic  8.87 us (3%)
    pallas_call x8, Pallas kernels, call(): pl.pallas_call(kernel, out_shape=out, in_specs=[VMEM] * len(args), out_sp...  196 us
    dot_general x6, matrix products, dot(): lax.dot_general(a, b, (((ca,), (cb,)), ((), ())), preferred_element_type=...  39.1 us
    all_gather x1, waiting for transfers between devices, local(): v_col = lax.all_gather(eigvecs.astype(bf16), 'feat', axis=0, tiled=True)  15.8 us
    all_gather x1, waiting for transfers between devices, local(): g_all = lax.all_gather(gc, 'feat', axis=1, tiled=True)  11.8 us
    transpose x1, local copies, waits for them, and re-layouts, local(): v_all = gather(v_col, 'rows', 2).transpose(1, 0, 2).reshape(d_all, d_all)  11.6 us
  transfers between devices with their start and end apart: 3, of which 2 were waited for; matrix products, arithmetic and copies ran while one was open for 22% of the time, Pallas kernels for 61%

profile of v1, /device:TPU:25, one launch (start us, length us, event | category | flops | bytes accessed | tf_op | source)
XLA Modules:
  0.0 323.9 jit_solution(7308609339603399277)
XLA Ops:
  6.5 1.9 convert_element_type.59
  10.2 6.4 %shard_map.55 = f32[8,8,512]{2,1,0:T(8,128)S(1)} custom-call(f32[8,512]{1,0:T(8,128)S(1)} %select_maximum_fusion.x_ref), custom_call_target="tpu_custom_call" | custom-call | flops 8000000000 | bytes 16384 | tf_op jit(solution)/shard_map/pallas_call | solution.py:108
  18.1 2.5 fusion.2
  20.6 15.8 %all-gather.8.cloned.1.call-done.x_ref = bf16[2048,256]{1,0:T(8,128)(2,1)} async-done(((bf16[512,256]{1,0:T(8,128)(2,1)}), bf16[2048,256]{1,0:T(8,128)(2,1)}) %all-gather.8.cloned.1.call-update) | async-done | bytes 1048592 | tf_op jit(solution)/shard_map/all_gather | solution.py:166
  37.6 56.1 %shard_map.56 = bf16[8,2048,256]{2,1,0:T(8,128)(2,1)} custom-call(bf16[2048,256]{1,0:T(8,128)(2,1)S(1)} %copy-done.5), custom_call_target="tpu_custom_call" | custom-call | flops 8000000000 | bytes 1048576 | tf_op jit(solution)/shard_map/pallas_call | solution.py:108
  93.7 11.6 %copy.8 = bf16[2048,8,256]{0,2,1:T(8,128)(2,1)} copy(bf16[2048,8,256]{2,0,1:T(8,128)(2,1)} %bitcast.49) | data formatting | bytes 16777216 | tf_op jit(solution)/shard_map/transpose | solution.py:173
  105.3 11.8 %all-gather.4.cloned.1.call-done = bf16[1024,2048]{1,0:T(8,128)(2,1)} async-done(((bf16[1024,512]{1,0:T(8,128)(2,1)}), bf16[1024,2048]{1,0:T(8,128)(2,1)}) %all-gather.4.cloned.1.call-update) | async-done | bytes 4194320 | tf_op jit(solution)/shard_map/all_gather | solution.py:172
  117.1 5.9 %convolution_convert_fusion = bf16[512,2048]{1,0:T(8,128)(2,1)} fusion(bf16[1024,512]{1,0:T(8,128)(2,1)S(1)} %copy-done.7, bf16[1024,2048]{1,0:T(8,128)(2,1)} %all-gather.4.cloned.1.call-done), kind=kOutput, calls=%fused_computation | convolution fusion | flops 2148532224 | bytes 7340032 | tf_op jit(solution)/shard_map/dot_general | solution.py:155
  123.0 3.9 %copy.9 = bf16[512,2048]{0,1:T(8,128)(2,1)} copy(bf16[512,2048]{1,0:T(8,128)(2,1)} %convolution_convert_fusion) | data formatting | bytes 4194304 | tf_op jit(solution)/shard_map/convert_element_type | solution.py:177
  126.9 4.2 %copy.10 = bf16[512,4,2,256]{3,0,1,2:T(8,128)(2,1)} copy(bf16[512,4,2,256]{0,3,2,1:T(8,128)(2,1)} %bitcast.50) | data formatting | bytes 4194304 | tf_op jit(solution)/shard_map/reshape | solution.py:178
  132.7 17.4 %shard_map.57.x_ref = bf16[512,256]{1,0:T(8,128)(2,1)S(1)} custom-call(bf16[2,4,512,256]{3,2,1,0:T(8,128)(2,1)S(1)} %bitcast.38), custom_call_target="tpu_custom_call" | custom-call | flops 8000000000 | bytes 2097152 | tf_op jit(solution)/shard_map/pallas_call | solution.py:108
  150.0 56.1 %shard_map.58 = bf16[4,512,256]{2,1,0:T(8,128)(2,1)S(1)} custom-call(bf16[512,256]{1,0:T(8,128)(2,1)S(1)} %shard_map.57.x_ref), custom_call_target="tpu_custom_call" | custom-call | flops 8000000000 | bytes 262144 | tf_op jit(solution)/shard_map/pallas_call | solution.py:108
  206.1 15.0 %shard_map.59 = bf16[8,256,256]{2,1,0:T(8,128)(2,1)S(1)} custom-call(bf16[8,256,256]{2,1,0:T(8,128)(2,1)S(1)} %bitcast.40), custom_call_target="tpu_custom_call" | custom-call | flops 8000000000 | bytes 1048576 | tf_op jit(solution)/shard_map/pallas_call | solution.py:108
  222.1 2.3 copy.11
  226.0 6.7 %fusion.1 = bf16[2048,256]{0,1:T(8,128)(2,1)} fusion(bf16[2048,256]{1,0:T(8,128)(2,1)S(1)} %bitcast.53, bf16[2048,2048]{0,1:T(8,128)(2,1)} %bitcast.46), kind=kOutput, calls=%fused_computation.9 | convolution fusion | flops 2148007936 | bytes 10485760 | tf_op jit(solution)/shard_map/dot_general | solution.py:155
  234.2 14.7 %shard_map.60 = bf16[8,256,256]{2,1,0:T(8,128)(2,1)S(1)} custom-call(bf16[8,256,256]{2,1,0:T(8,128)(2,1)S(1)} %bitcast.43), custom_call_target="tpu_custom_call" | custom-call | flops 8000000000 | bytes 1048576 | tf_op jit(solution)/shard_map/pallas_call | solution.py:108
  251.4 11.6 %convolution_convert_fusion.1 = bf16[256,2048]{1,0:T(8,128)(2,1)} fusion(bf16[2048,2048]{0,1:T(8,128)(2,1)} %bitcast.47, bf16[256,2048]{0,1:T(8,128)(2,1)S(1)} %bitcast.54, f32[2048]{0:T(1024)S(1)} %copy-done.8, f32[256]{0:T(256)S(1)} %get-tuple-element.10, f32[2048]{0:T(1024)S(1)} %broadcast_power_fusion, f32[256]{0:T(256)S(1)} %broadcast_power_fusion.1, ...), kind=kOutput, calls=%fused_computation.7 | convolution fusion | flops 4299685888 | bytes 10506240 | tf_op jit(solution)/shard_map/dot_general | solution.py:155
  263.0 2.3 copy.14
  266.7 14.7 %shard_map.61 = bf16[8,256,256]{2,1,0:T(8,128)(2,1)S(1)} custom-call(bf16[8,256,256]{2,1,0:T(8,128)(2,1)S(1)} %bitcast.45), custom_call_target="tpu_custom_call" | custom-call | flops 8000000000 | bytes 1048576 | tf_op jit(solution)/shard_map/pallas_call | solution.py:108
  281.5 2.4 fusion.11.x_ref
  283.8 15.7 %shard_map.62 = bf16[8,512,256]{2,1,0:T(8,128)(2,1)S(1)} custom-call(bf16[512,256]{1,0:T(8,128)(2,1)S(1)} %fusion.11.x_ref), custom_call_target="tpu_custom_call" | custom-call | flops 8000000000 | bytes 262144 | tf_op jit(solution)/shard_map/pallas_call | solution.py:108
  300.9 3.9 %copy.16 = bf16[512,8,256]{0,2,1:T(8,128)(2,1)} copy(bf16[512,8,256]{2,0,1:T(8,128)(2,1)} %bitcast.39) | data formatting | bytes 4194304 | tf_op jit(solution)/shard_map/transpose | solution.py:194
  304.8 5.8 %fusion.17 = f32[1024,512]{1,0:T(8,128)} fusion(bf16[1024,2048]{1,0:T(8,128)(2,1)} %all-gather.4.cloned.1.call-done, bf16[2048,512]{1,0:T(8,128)(2,1)S(1)} %copy-done), kind=kOutput, calls=%fused_computation.31 | convolution fusion | flops 2147483648 | bytes 8388608 | tf_op jit(solution)/shard_map/dot_general | solution.py:155
  310.6 6.7 %add_convert_fusion = bf16[1024,512]{1,0:T(8,128)(2,1)} fusion(f32[1024,512]{1,0:T(8,128)} %fusion.17, bf16[1024,2048]{1,0:T(8,128)(2,1)} %all-gather.6.cloned.1.call-done, bf16[512,2048]{0,1:T(8,128)(2,1)} %bitcast.52), kind=kOutput, calls=%fused_computation.15 | convolution fusion | flops 2148532224 | bytes 9437184 | tf_op jit(solution)/shard_map/dot_general | solution.py:155
  (40 shorter events, 15.1 us)
Async XLA Ops:
  6.5 298.3 %copy-start = (bf16[2048,512]{1,0:T(8,128)(2,1)S(1)}, bf16[2048,512]{1,0:T(8,128)(2,1)}, u32[]{:S(2)}) copy-start(bf16[2048,512]{1,0:T(8,128)(2,1)} %param.9) | copy-start | bytes 6291460
  6.5 3.4 %copy-start.6 = (bf16[1024,512]{1,0:T(8,128)(2,1)S(1)}, bf16[1024,512]{1,0:T(8,128)(2,1)}, u32[]{:S(2)}) copy-start(bf16[1024,512]{1,0:T(8,128)(2,1)} %param.6) | copy-start | bytes 3145732
  6.5 29.8 %all-gather.8.cloned.1.call-start = ((), (), s32[]{:S(2)}) async-start(), calls=%async_computation.2 | async-start | bytes 1310720 | tf_op jit(solution)/shard_map/all_gather | solution.py:166
  8.5 108.6 %all-gather.4.cloned.1.call-start = ((), (), s32[]{:S(2)}) async-start(), calls=%async_computation | async-start | bytes 5242880 | tf_op jit(solution)/shard_map/all_gather | solution.py:172
  16.7 1.3 copy-start.8
  17.9 292.7 %all-gather.6.cloned.1.call-start = ((), (), s32[]{:S(2)}) async-start(), calls=%async_computation.1 | async-start | bytes 5242880 | tf_op jit(solution)/shard_map/all_gather | solution.py:176
  36.4 1.2 copy-start.5
  93.7 23.4 %copy-start.7 = (bf16[1024,512]{1,0:T(8,128)(2,1)S(1)}, bf16[1024,512]{1,0:T(8,128)(2,1)}, u32[]{:S(2)}) copy-start(bf16[1024,512]{1,0:T(8,128)(2,1)} %fusion.2) | copy-start | bytes 3145732
  131.1 1.6 copy-start.1
  221.2 1.0 copy-start.4
  248.9 1.0 copy-start.3
  299.6 1.3 copy-start.2
Sparse Core Ops, SparseCore 0:
  8.9 27.4 all-gather.7
  38.0 79.0 all-gather.3
  118.6 101.4 all-gather.5

commit v2 on v1

--- a/solution.py
+++ b/solution.py
@@ -137,6 +137,170 @@
     return call(functools.partial(scatter_kernel, axis, n), jax.ShapeDtypeStruct(piece, bf16), scratch, cid, x.nbytes, x)
 
 
+def lanes(index, width):
+    return pl.ds(pl.multiple_of(index * width, width), width)
+
+
+def chain_kernel(n, zn, scale, x_ref, v_ref, k_ref, o_ref, landed, stage, parts, c_col, turned, rows,
+                 t_out, t_in, spread, n_out, n_in, own_q, rs, zs, ss, ts, ns, gs):
+    me, z = lax.axis_index("rows"), lax.axis_index("feat")
+    core, chip = lax.rem(me, 2), me // 2
+    mate = me + 1 - 2 * core
+    h, per = n // 2, n // zn
+    nar = t_out.shape[1]
+    own = x_ref.shape[0]
+    barrier = pltpu.get_barrier_semaphore()
+    for d in range(1, n):
+        pl.semaphore_signal(barrier, inc=1, device_id={"rows": lax.rem(me + d, n)}, device_id_type=MESH)
+    for d in range(1, zn):
+        pl.semaphore_signal(barrier, inc=1, device_id={"feat": lax.rem(z + d, zn)}, device_id_type=MESH)
+    pl.semaphore_wait(barrier, n + zn - 2)
+
+    pending = []
+    core_copies = []
+    order = list(range(1, h)) + [0]
+    for d in order:
+        piece = 2 * lax.rem(chip + d, h) + 1 - core
+        copy = remote(x_ref.at[:, lanes(piece, nar)], landed.at[d], rs[0].at[d], rs[1].at[d], "rows", mate)
+        copy.start()
+        core_copies.append(copy)
+    copies = []
+    for i, d in enumerate(order):
+        piece = 2 * lax.rem(chip + d, h) + core
+        core_copies[i].wait_recv()
+        both = x_ref[:, lanes(piece, nar)].astype(f32) + landed[d].astype(f32)
+        if d:
+            stage[d] = both.astype(bf16)
+            copy = remote(stage.at[d], parts.at[d], rs[2].at[d], rs[3].at[d], "rows", lax.rem(me + 2 * d, n))
+            copy.start()
+            copies.append(copy)
+    for d in range(1, h):
+        copies[d - 1].wait_recv()
+        both = both + parts[d].astype(f32)
+    c_col[z] = both.astype(bf16)
+    pending += core_copies + copies
+
+    def pass_tiles(block):
+        for i in range(per):
+            s = block * per + i
+            off = lax.rem(s - me + n, n)
+
+            @pl.when(off != 0)
+            def _():
+                remote(c_col.at[block, pl.ds(i * nar, nar)], turned.at[me], ss[0].at[off - 1], ss[1].at[off - 1], "rows", s).start()
+
+            @pl.when(off == 0)
+            def _():
+                turned[me] = c_col[block, pl.ds(i * nar, nar)]
+
+    z_copies = []
+    for d in range(1, zn):
+        copy = remote(c_col.at[z], c_col.at[z], zs[0].at[d - 1], zs[1].at[d - 1], "feat", lax.rem(z + d, zn))
+        copy.start()
+        z_copies.append(copy)
+    pass_tiles(z)
+    for d in range(1, zn):
+        z_copies[d - 1].wait_recv()
+        pass_tiles(lax.rem(z + zn - d, zn))
+    pending += z_copies
+
+    def add_rows(source):
+        inner = c_col[source // per, pl.ds(pl.multiple_of(lax.rem(source, per) * nar, nar), nar)]
+        both = 0.5 * (turned[source].astype(f32) + inner.astype(f32).T)
+        rows[:, lanes(source, nar)] = both.astype(bf16)
+
+    for d in range(n):
+        source = lax.rem(me + n - d, n)
+        if d:
+            copy = remote(c_col.at[0, pl.ds(0, nar)], turned.at[source], ss[0].at[d - 1], ss[1].at[d - 1], "rows", lax.rem(me + d, n))
+            copy.wait_recv()
+            pending.append(copy)
+        add_rows(source)
+
+    def swap(make, outs, ins, sems):
+        copies = []
+        for d in list(range(1, n)) + [0]:
+            s = lax.rem(me + d, n)
+            piece = make(s).astype(bf16)
+            if d:
+                outs[s] = piece
+                copy = remote(outs.at[s], ins.at[me], sems[0].at[d - 1], sems[1].at[d - 1], "rows", s)
+                copy.start()
+                copies.append(copy)
+            else:
+                ins[me] = piece
+        return copies
+
+    t_copies = swap(lambda s: jnp.dot(rows[...], v_ref[s], preferred_element_type=f32), t_out, t_in, ts)
+    for d in range(n):
+        source = lax.rem(me + n - d, n)
+        if d:
+            t_copies[d - 1].wait_recv()
+        spread[:, lanes(source, nar)] = t_in[source].astype(f32).T.astype(bf16)
+    pending += t_copies
+    for q in range(n):
+        block = jnp.dot(spread[...], v_ref[q], preferred_element_type=f32)
+        rows[:, pl.ds(q * nar, nar)] = (k_ref[:, pl.ds(q * nar, nar)] * block).astype(bf16)
+
+    def back(s):
+        total = None
+        for q in range(n):
+            term = lax.dot_general(
+                rows[:, pl.ds(q * nar, nar)], v_ref[q, pl.ds(pl.multiple_of(s * nar, nar), nar)],
+                (((1,), (1,)), ((), ())), preferred_element_type=f32,
+            )
+            total = term if total is None else total + term
+        return total
+
+    n_copies = swap(back, n_out, n_in, ns)
+    pending += n_copies
+    total = None
+    for d in range(n):
+        source = lax.rem(me + n - d, n)
+        if d:
+            n_copies[d - 1].wait_recv()
+        left = v_ref[source, pl.ds(pl.multiple_of(z * own, own), own)]
+        term = jnp.dot(left, n_in[source], preferred_element_type=f32)
+        total = term if total is None else total + term
+    own_q[...] = (scale * total).astype(bf16)
+
+    copies, passed = [], []
+    mine = o_ref.at[:, lanes(me, nar)]
+    for d in range(1, h):
+        copy = remote(own_q, mine, gs[0].at[d], gs[1].at[d], "rows", lax.rem(me + 2 * d, n))
+        copy.start()
+        copies.append(copy)
+    passed.append(remote(own_q, mine, gs[2].at[0], gs[3].at[0], "rows", mate))
+    passed[0].start()
+    o_ref[:, lanes(me, nar)] = own_q[...]
+    for d in range(1, h):
+        there = o_ref.at[:, lanes(lax.rem(me + n - 2 * d, n), nar)]
+        copies[d - 1].wait_recv()
+        copy = remote(there, there, gs[2].at[d], gs[3].at[d], "rows", mate)
+        copy.start()
+        passed.append(copy)
+    for copy in passed:
+        copy.wait()
+    for copy in copies + pending:
+        copy.wait_send()
+
+
+def chain(part, v_pieces, kernel_rows, row_count):
+    n, zn = lax.axis_size("rows"), lax.axis_size("feat")
+    own, d_all = part.shape
+    nar, h = d_all // n, n // 2
+    tile, square = (h, own, nar), (n, nar, nar)
+    dma = pltpu.SemaphoreType.DMA
+    scratch = [pltpu.VMEM(tile, bf16)] * 3 + [pltpu.VMEM((zn, own, nar), bf16), pltpu.VMEM(square, bf16)]
+    scratch += [pltpu.VMEM((nar, d_all), bf16), pltpu.VMEM(square, bf16), pltpu.VMEM(square, bf16)]
+    scratch += [pltpu.VMEM((nar, d_all), bf16), pltpu.VMEM(square, bf16), pltpu.VMEM(square, bf16)]
+    scratch += [pltpu.VMEM((own, nar), bf16)]
+    scratch += [[dma((h,))] * 4, [dma((zn - 1,))] * 2, [dma((n - 1,))] * 2, [dma((n - 1,))] * 2]
+    scratch += [[dma((n - 1,))] * 2, [dma((h,))] * 4]
+    kernel = functools.partial(chain_kernel, n, zn, 2.0 / row_count)
+    return call(kernel, jax.ShapeDtypeStruct((own, d_all), bf16), scratch, 9, 8 * part.nbytes, part, v_pieces, kernel_rows)
+
+
 def divided(lam_row, lam_col, first_row):
     on_diag = (
         (first_row + jnp.arange(lam_row.shape[0], dtype=jnp.int32))[:, None]
@@ -155,6 +319,26 @@
     return lax.dot_general(a, b, (((ca,), (cb,)), ((), ())), preferred_element_type=f32)
 
 
+def chain_by_calls(part, v_pieces, kernel_rows, row_count):
+    n = lax.axis_size("rows")
+    own, d_all = part.shape
+    nar = d_all // n
+    v_all = v_pieces.transpose(1, 0, 2).reshape(d_all, d_all)
+    part = part.reshape(own, n // 2, 2, nar).transpose(2, 1, 0, 3)
+    tile = scatter(part, "rows", 3)
+    c_col = exchange(tile, "feat", 4, same=True).reshape(n, nar, nar)
+    turned = exchange(c_col, "rows", 5)
+    both = 0.5 * (c_col.astype(f32) + turned.transpose(0, 2, 1).astype(f32))
+    half = dot(v_all, both.reshape(d_all, nar).astype(bf16), 0, 0).astype(bf16)
+    half = exchange(half.reshape(n, nar, nar), "rows", 6)
+    rotated = dot(half.transpose(1, 0, 2).reshape(nar, d_all), v_all, 1, 0)
+    back = dot((kernel_rows * rotated).astype(bf16), v_all, 1, 1).astype(bf16)
+    back = exchange(back.reshape(nar, n, nar).transpose(1, 0, 2), "rows", 7).reshape(d_all, nar)
+    v_own = lax.dynamic_slice_in_dim(v_all, lax.axis_index("feat") * own, own)
+    sens = (2.0 / row_count * dot(v_own, back, 1, 0)).astype(bf16)
+    return gather(sens, "rows", 8).transpose(1, 0, 2).reshape(own, d_all)
+
+
 def local(features, grad_out, eigvecs, eigvals, whiten):
     tok_rows, own = features.shape
     n = lax.axis_size("rows")
@@ -170,28 +354,17 @@
     xc = (features.astype(f32) - means[0]).astype(bf16)
     gc = (grad_out.astype(f32) - means[1]).astype(bf16)
     g_all = lax.all_gather(gc, "feat", axis=1, tiled=True)
-    v_all = gather(v_col, "rows", 2).transpose(1, 0, 2).reshape(d_all, d_all)
-
+    v_pieces = gather(v_col, "rows", 2)
+    first = me * nar
+    lam_row = lax.dynamic_slice_in_dim(eigvals, first, nar)
+    kernel_rows = divided(lam_row, eigvals, first)
     xc, g_all = lax.optimization_barrier((xc, g_all))
     x_all = lax.all_gather(xc, "feat", axis=1, tiled=True)
     part = dot(xc, g_all, 0, 0).astype(bf16)
-    part = part.reshape(own, n // 2, 2, nar).transpose(2, 1, 0, 3)
-    tile = scatter(part, "rows", 3)
-    c_col = exchange(tile, "feat", 4, same=True).reshape(n, nar, nar)
-    turned = exchange(c_col, "rows", 5)
-    both = 0.5 * (c_col.astype(f32) + turned.transpose(0, 2, 1).astype(f32))
-    both = both.reshape(d_all, nar).astype(bf16)
-    half = dot(v_all, both, 0, 0).astype(bf16)
-    half = exchange(half.reshape(n, nar, nar), "rows", 6)
-    rotated = dot(half.transpose(1, 0, 2).reshape(nar, d_all), v_all, 1, 0)
-    first = me * nar
-    lam_row = lax.dynamic_slice_in_dim(eigvals, first, nar)
-    scaled = (divided(lam_row, eigvals, first) * rotated).astype(bf16)
-    back = dot(scaled, v_all, 1, 1).astype(bf16)
-    back = exchange(back.reshape(nar, n, nar).transpose(1, 0, 2), "rows", 7).reshape(d_all, nar)
-    v_own = lax.dynamic_slice_in_dim(v_all, lax.axis_index("feat") * own, own)
-    sens = (2.0 / row_count * dot(v_own, back, 1, 0)).astype(bf16)
-    sens = gather(sens, "rows", 8).transpose(1, 0, 2).reshape(own, d_all)
+    if nar % 128 == 0:
+        sens = chain(part, v_pieces, kernel_rows, row_count)
+    else:
+        sens = chain_by_calls(part, v_pieces, kernel_rows, row_count)
     grad_in = dot(g_all, whiten, 1, 0) + dot(x_all, sens, 1, 1)
     return grad_in.astype(bf16)
 

time: 325 us -> 312 us (0.960)
  waiting for transfers between devices: 27.6 us -> 102 us
  local copies, waits for them, and re-layouts: 38.7 us -> 2.6 us
  matrix products: 39.1 us -> 12.8 us
  Pallas kernels: 196 us -> 171 us
    all_gather x1, waiting for transfers between devices: 11.8 us -> 75.5 us  [local(): g_all = lax.all_gather(gc, 'feat', axis=1, tiled=True)]
    dot_general x6 -> x3, matrix products: 39.1 us -> 12.8 us  [dot(): lax.dot_general(a, b, (((ca,), (cb,)), ((), ())), preferred_element_type=...]
    pallas_call x8 -> x3, Pallas kernels: 196 us -> 171 us  [call(): pl.pallas_call(kernel, out_shape=out, in_specs=[VMEM] * len(args), out_sp...]
    transpose x3 -> x0, local copies, waits for them, and re-layouts: 17 us -> none  [the longest x1 11.6 us: local(): v_all = gather(v_col, 'rows', 2).transpose(1, 0, 2).reshape(d_all, d_all)]
    all_gather x1, waiting for transfers between devices: 15.8 us -> 26.7 us  [local(): v_col = lax.all_gather(eigvecs.astype(bf16), 'feat', axis=0, tiled=True)]
    convert_element_type x3 -> x0, local copies, waits for them, and re-layouts: 7.69 us -> none  [the longest x1 3.91 us: local(): part = dot(xc, g_all, 0, 0).astype(bf16)]
    reshape x2 -> x0, local copies, waits for them, and re-layouts: 5.66 us -> none  [the longest x1 4.18 us: local(): part = part.reshape(own, n // 2, 2, nar).transpose(2, 1, 0, 3)]
    unnamed x18 -> x16, local copies, waits for them, and re-layouts: 6.05 us -> 2.58 us
  transfers between devices with their start and end apart: 3 -> 3, of which waited for: 2 -> 2; matrix products, arithmetic and copies ran while one was open for 22% -> 4% of each run, Pallas kernels for 61% -> 53%
where the time goes in v2:
time: 312 us; the launch traced here: 311 us
  Pallas kernels  171 us (55%)
  waiting for transfers between devices  102 us (33%)
  between operations  13.3 us (4%)
  matrix products  12.8 us (4%)
  other arithmetic  9.55 us (3%)
    pallas_call x3, Pallas kernels, call(): pl.pallas_call(kernel, out_shape=out, in_specs=[VMEM] * len(args), out_sp...  171 us
    all_gather x1, waiting for transfers between devices, local(): g_all = lax.all_gather(gc, 'feat', axis=1, tiled=True)  75.5 us
    all_gather x1, waiting for transfers between devices, local(): v_col = lax.all_gather(eigvecs.astype(bf16), 'feat', axis=0, tiled=True)  26.7 us
    dot_general x3, matrix products, dot(): lax.dot_general(a, b, (((ca,), (cb,)), ((), ())), preferred_element_type=...  12.8 us
  transfers between devices with their start and end apart: 3, of which 2 were waited for; matrix products, arithmetic and copies ran while one was open for 4% of the time, Pallas kernels for 53%

profile of v2, /device:TPU:25, one launch (start us, length us, event | category | flops | bytes accessed | tf_op | source)
XLA Modules:
  0.0 311.3 jit_solution(7985152557575562169)
XLA Ops:
  6.5 1.6 convert_reduce_fusion.1
  8.1 1.4 convert_reduce_fusion
  9.6 0.0 copy-start.3
  9.6 6.4 %shard_map.55 = f32[8,8,512]{2,1,0:T(8,128)S(1)} custom-call(f32[8,512]{1,0:T(8,128)S(1)} %select_maximum_fusion.x_ref), custom_call_target="tpu_custom_call" | custom-call | flops 8000000000 | bytes 16384 | tf_op jit(solution)/shard_map/pallas_call | solution.py:108
  16.1 1.2 fusion.1
  17.3 0.0 all-gather.4.cloned.1.call-update
  17.3 0.0 copy-start.6
  17.3 0.0 all-gather.8.cloned.1.call-start
  17.4 1.8 convert_element_type.30
  19.2 0.0 all-gather.8.cloned.1.call-update
  19.3 0.0 all-gather.6.cloned.1.call-start
  19.3 1.2 fusion
  20.5 75.5 %all-gather.4.cloned.1.call-done = bf16[1024,2048]{1,0:T(8,128)(2,1)} async-done(((bf16[1024,512]{1,0:T(8,128)(2,1)}), bf16[1024,2048]{1,0:T(8,128)(2,1)}) %all-gather.4.cloned.1.call-update) | async-done | bytes 4194320 | tf_op jit(solution)/shard_map/all_gather | solution.py:356
  96.0 0.0 all-gather.6.cloned.1.call-update
  96.1 0.1 power_multiply_fusion
  96.2 2.1 divide_select_fusion.k_ref
  98.3 26.7 %all-gather.8.cloned.1.call-done.x_ref = bf16[2048,256]{1,0:T(8,128)(2,1)} async-done(((bf16[512,256]{1,0:T(8,128)(2,1)}), bf16[2048,256]{1,0:T(8,128)(2,1)}) %all-gather.8.cloned.1.call-update) | async-done | bytes 1048592 | tf_op jit(solution)/shard_map/all_gather | solution.py:350
  125.0 1.2 copy-done.1
  126.2 56.2 %shard_map.56.v_ref = bf16[8,2048,256]{2,1,0:T(8,128)(2,1)} custom-call(bf16[2048,256]{1,0:T(8,128)(2,1)S(1)} %copy-done.1), custom_call_target="tpu_custom_call" | custom-call | flops 8000000000 | bytes 1048576 | tf_op jit(solution)/shard_map/pallas_call | solution.py:108
  182.4 2.4 convolution_convert_fusion.x_ref
  184.8 3.7 %fusion.3 = f32[1024,512]{1,0:T(8,128)} fusion(bf16[1024,2048]{1,0:T(8,128)(2,1)S(1)} %copy-done.7, bf16[2048,512]{1,0:T(8,128)(2,1)S(1)} %copy-done), kind=kOutput, calls=%fused_computation.18 | convolution fusion | flops 2147483648 | bytes 8388608 | tf_op jit(solution)/shard_map/dot_general | solution.py:319
  188.5 108.2 %shard_map.57 = bf16[512,2048]{1,0:T(8,128)(2,1)S(1)} custom-call(bf16[512,2048]{1,0:T(8,128)(2,1)S(1)} %convolution_convert_fusion.x_ref, bf16[8,2048,256]{2,1,0:T(8,128)(2,1)} %shard_map.56.v_ref, f32[256,2048]{1,0:T(8,128)} %divide_select_fusion.k_ref), custom_call_target="tpu_custom_call" | custom-call | flops 8000000000 | bytes 16777216 | tf_op jit(solution)/shard_map/pallas_call | solution.py:108
  296.7 1.3 copy-done.2
  298.0 6.8 %add_convert_fusion = bf16[1024,512]{1,0:T(8,128)(2,1)} fusion(f32[1024,512]{1,0:T(8,128)} %fusion.3, bf16[1024,2048]{1,0:T(8,128)(2,1)} %all-gather.6.cloned.1.call-done, bf16[512,2048]{1,0:T(8,128)(2,1)} %copy-done.2), kind=kOutput, calls=%fused_computation.7 | convolution fusion | flops 2148532224 | bytes 9437184 | tf_op jit(solution)/shard_map/dot_general | solution.py:319
  (21 shorter events, 0.1 us)
Async XLA Ops:
  6.5 178.3 %copy-start = (bf16[2048,512]{1,0:T(8,128)(2,1)S(1)}, bf16[2048,512]{1,0:T(8,128)(2,1)}, u32[]{:S(2)}) copy-start(bf16[2048,512]{1,0:T(8,128)(2,1)} %param.9) | copy-start | bytes 6291460
  6.5 89.5 %all-gather.4.cloned.1.call-start = ((), (), s32[]{:S(2)}) async-start(), calls=%async_computation | async-start | bytes 5242880 | tf_op jit(solution)/shard_map/all_gather | solution.py:356
  9.6 6.5 %copy-start.3 = (bf16[1024,512]{1,0:T(8,128)(2,1)S(1)}, bf16[1024,512]{1,0:T(8,128)(2,1)}, u32[]{:S(2)}) copy-start(bf16[1024,512]{1,0:T(8,128)(2,1)} %param.6) | copy-start | bytes 3145732
  17.3 2.0 copy-start.4
  17.3 78.7 %copy-start.6 = (f32[2048]{0:T(1024)S(1)}, f32[2048]{0:T(1024)}, u32[]{:S(2)}) copy-start(f32[2048]{0:T(1024)} %param.8) | copy-start | bytes 24580
  17.3 107.7 %all-gather.8.cloned.1.call-start = ((), (), s32[]{:S(2)}) async-start(), calls=%async_computation.2 | async-start | bytes 1310720 | tf_op jit(solution)/shard_map/all_gather | solution.py:350
  19.3 278.8 %all-gather.6.cloned.1.call-start = ((), (), s32[]{:S(2)}) async-start(), calls=%async_computation.1 | async-start | bytes 5242880 | tf_op jit(solution)/shard_map/all_gather | solution.py:362
  125.0 1.2 copy-start.1
  126.2 56.2 %copy-start.5 = (bf16[1024,512]{1,0:T(8,128)(2,1)S(1)}, bf16[1024,512]{1,0:T(8,128)(2,1)}, u32[]{:S(2)}) copy-start(bf16[1024,512]{1,0:T(8,128)(2,1)} %fusion) | copy-start | bytes 3145732
  126.2 56.2 %copy-start.7 = (bf16[1024,2048]{1,0:T(8,128)(2,1)S(1)}, bf16[1024,2048]{1,0:T(8,128)(2,1)}, u32[]{:S(2)}) copy-start(bf16[1024,2048]{1,0:T(8,128)(2,1)} %all-gather.4.cloned.1.call-done) | copy-start | bytes 12582916
  296.7 1.3 copy-start.2
Sparse Core Ops, SparseCore 0:
  17.4 78.5 all-gather.3
  97.6 27.3 all-gather.7
  126.6 79.1 all-gather.5

commit v3 on v2

--- a/solution.py
+++ b/solution.py
@@ -109,7 +109,7 @@
         kernel,
         out_shape=out,
         in_specs=[VMEM] * len(args),
-        out_specs=VMEM,
+        out_specs=jax.tree.map(lambda _: VMEM, out),
         scratch_shapes=scratch,
         compiler_params=pltpu.CompilerParams(collective_id=cid, has_side_effects=True, vmem_limit_bytes=48 * 2**20),
         cost_estimate=pl.CostEstimate(flops=8_000_000_000, bytes_accessed=sent, transcendentals=0),
@@ -299,6 +299,120 @@
     scratch += [[dma((n - 1,))] * 2, [dma((h,))] * 4]
     kernel = functools.partial(chain_kernel, n, zn, 2.0 / row_count)
     return call(kernel, jax.ShapeDtypeStruct((own, d_all), bf16), scratch, 9, 8 * part.nbytes, part, v_pieces, kernel_rows)
+
+
+def front_kernel(n, zn, chunks, g_ref, v_ref, g_out, v_out, send, recv, near, far, mate_send, mate_recv):
+    me, z = lax.axis_index("rows"), lax.axis_index("feat")
+    core = lax.rem(me, 2)
+    mate = me + 1 - 2 * core
+    h = n // 2
+    own, ck = v_ref.shape[0], g_ref.shape[0] // chunks
+    units = chunks + 1
+    peers = [lax.rem(me + 2 * d, n) for d in range(1, h)]
+    barrier = pltpu.get_barrier_semaphore()
+    for target in [mate] + peers:
+        pl.semaphore_signal(barrier, inc=1, device_id={"rows": target}, device_id_type=MESH)
+    for d in range(1, zn):
+        pl.semaphore_signal(barrier, inc=1, device_id={"feat": lax.rem(z + d, zn)}, device_id_type=MESH)
+    pl.semaphore_wait(barrier, h + zn - 1)
+
+    def there(block, unit):
+        if unit == 0:
+            return v_out.at[me, pl.ds(pl.multiple_of(block * own, own), own)]
+        return g_out.at[pl.ds((unit - 1) * ck, ck), lanes(block, own)]
+
+    def hop(way, step, unit):
+        block = z - step if way == 0 else z + step
+        if step == 0:
+            src = v_ref if unit == 0 else g_ref.at[pl.ds((unit - 1) * ck, ck)]
+        else:
+            src = there(block, unit)
+        target = lax.rem(z + (1 if way == 0 else zn - 1), zn)
+        return remote(src, there(block, unit), send.at[way, step, unit], recv.at[way, step, unit], "feat", target)
+
+    def held(way, step):
+        return z >= step if way == 0 else z + step < zn
+
+    def onward(way):
+        return z < zn - 1 if way == 0 else z > 0
+
+    def spread(block, d, fresh=False):
+        src = v_ref if fresh else there(block, 0)
+        return remote(src, there(block, 0), near.at[block, d], far.at[block, d], "rows", peers[d - 1])
+
+    def to_mate(block, d, fresh=False):
+        source = lax.rem(me + n - 2 * d, n) if d else me
+        ref = v_out.at[source, pl.ds(pl.multiple_of(block * own, own), own)]
+        src = v_ref if fresh else ref
+        return remote(src, ref, mate_send.at[block, d], mate_recv.at[block, d], "rows", mate)
+
+    def spread_all(block, fresh=False):
+        for d in range(1, h):
+            spread(block, d, fresh).start()
+        to_mate(block, 0, fresh).start()
+
+    def pass_mate(block):
+        for d in range(1, h):
+            spread(block, d).wait_recv()
+            to_mate(block, d).start()
+
+    def each(step, what):
+        if step == 0:
+            what(z)
+            return
+        for way in (0, 1):
+            @pl.when(held(way, step))
+            def _():
+                what(z - step if way == 0 else z + step)
+
+    for unit in range(units):
+        for way in (0, 1):
+            @pl.when(onward(way))
+            def _():
+                hop(way, 0, unit).start()
+    spread_all(z, True)
+    v_out[me, pl.ds(pl.multiple_of(z * own, own), own)] = v_ref[...]
+    g_out[:, lanes(z, own)] = g_ref[...]
+    for step in range(1, zn):
+        for unit in range(units):
+            for way in (0, 1):
+                @pl.when(held(way, step))
+                def _():
+                    hop(way, step - 1, unit).wait_recv()
+                    if step < zn - 1:
+                        @pl.when(onward(way))
+                        def _():
+                            hop(way, step, unit).start()
+                    if unit == 0:
+                        spread_all(z - step if way == 0 else z + step)
+        each(step - 1, pass_mate)
+    each(zn - 1, pass_mate)
+
+    def finish(block):
+        for d in range(1, h):
+            spread(block, d).wait_send()
+        for d in range(h):
+            to_mate(block, d).wait()
+
+    for step in range(zn):
+        each(step, finish)
+    for step in range(zn - 1):
+        for unit in range(units):
+            for way in (0, 1):
+                @pl.when(jnp.logical_and(held(way, step), onward(way)))
+                def _():
+                    hop(way, step, unit).wait_send()
+
+
+def front(g, v):
+    n, zn = lax.axis_size("rows"), lax.axis_size("feat")
+    tok, own = g.shape
+    chunks = 4
+    dma = pltpu.SemaphoreType.DMA
+    out = (jax.ShapeDtypeStruct((tok, own * zn), bf16), jax.ShapeDtypeStruct((n, own * zn, v.shape[1]), bf16))
+    scratch = [dma((2, zn - 1, chunks + 1))] * 2 + [dma((zn, n // 2))] * 4
+    kernel = functools.partial(front_kernel, n, zn, chunks)
+    return call(kernel, out, scratch, 10, zn * g.nbytes, g, v)
 
 
 def divided(lam_row, lam_col, first_row):
@@ -347,14 +461,12 @@
     row_count = tok_rows * n
     me = lax.axis_index("rows")
 
-    v_col = lax.all_gather(eigvecs.astype(bf16), "feat", axis=0, tiled=True)
     sums = jnp.stack([jnp.sum(features, axis=0, dtype=f32), jnp.sum(grad_out, axis=0, dtype=f32)])
     sums = jnp.pad(sums, ((0, 6), (0, 0)))
     means = jnp.sum(gather(sums, "rows", 1), axis=0) / row_count
     xc = (features.astype(f32) - means[0]).astype(bf16)
     gc = (grad_out.astype(f32) - means[1]).astype(bf16)
-    g_all = lax.all_gather(gc, "feat", axis=1, tiled=True)
-    v_pieces = gather(v_col, "rows", 2)
+    g_all, v_pieces = front(gc, eigvecs.astype(bf16))
     first = me * nar
     lam_row = lax.dynamic_slice_in_dim(eigvals, first, nar)
     kernel_rows = divided(lam_row, eigvals, first)

time: 312 us -> 279 us (0.89)
  waiting for transfers between devices: 102 us -> 0.02 us
  Pallas kernels: 171 us -> 239 us
    all_gather x2 -> x0, waiting for transfers between devices: 102 us -> none  [the longest x1 75.5 us: local(): g_all = lax.all_gather(gc, 'feat', axis=1, tiled=True)]
    pallas_call x3, Pallas kernels: 171 us -> 239 us  [call(): pl.pallas_call(kernel, out_shape=out, in_specs=[VMEM] * len(args), out_sp...]
  transfers between devices with their start and end apart: 3 -> 1, of which waited for: 2 -> 0; matrix products, arithmetic and copies ran while one was open for 4% -> 4% of each run, Pallas kernels for 53% -> 49%
where the time goes in v3:
time: 279 us
  Pallas kernels  239 us (86%)
  matrix products  15.2 us (5%)
  between operations  13.5 us (5%)
  other arithmetic  8.01 us (3%)
  local copies, waits for them, and re-layouts  3.39 us (1%)
    pallas_call x3, Pallas kernels, call(): pl.pallas_call(kernel, out_shape=out, in_specs=[VMEM] * len(args), out_sp...  239 us
    dot_general x3, matrix products, dot(): lax.dot_general(a, b, (((ca,), (cb,)), ((), ())), preferred_element_type=...  15.2 us
  transfers between devices with their start and end apart: 1, of which 0 were waited for; matrix products, arithmetic and copies ran while one was open for 4% of the time, Pallas kernels for 49%

profile of v3, /device:TPU:25, one launch (start us, length us, event | category | flops | bytes accessed | tf_op | source)
XLA Modules:
  0.0 279.1 jit_solution(12298432668326066076)
XLA Ops:
  6.5 0.0 copy-start
  6.5 0.0 all-gather.2.cloned.1.call-start
  6.5 1.6 convert_reduce_fusion.1
  8.1 1.4 convert_reduce_fusion
  9.6 6.4 %shard_map.55 = f32[8,8,512]{2,1,0:T(8,128)S(1)} custom-call(f32[8,512]{1,0:T(8,128)S(1)} %select_maximum_fusion.x_ref), custom_call_target="tpu_custom_call" | custom-call | flops 8000000000 | bytes 16384 | tf_op jit(solution)/shard_map/pallas_call | solution.py:108
  16.0 0.0 copy-start.6
  16.1 0.0 copy-start.4
  16.1 1.5 fusion.1.g_ref
  17.6 0.0 copy-done.6
  17.7 0.1 copy-done.4
  17.7 1.2 fusion
  18.9 95.4 %shard_map.56 = (bf16[1024,2048]{1,0:T(8,128)(2,1)S(1)}, bf16[8,2048,256]{2,1,0:T(8,128)(2,1)}) custom-call(bf16[1024,512]{1,0:T(8,128)(2,1)S(1)} %fusion.1.g_ref, bf16[512,256]{1,0:T(8,128)(2,1)S(1)} %convert_element_type.29.v_ref), custom_call_target="tpu_custom_call" | custom-call | flops 8000000000 | bytes 4194304 | tf_op jit(solution)/shard_map/pallas_call | solution.py:108
  114.3 0.0 copy-start.1
  114.3 1.9 copy-done.1
  116.3 0.0 all-gather.2.cloned.1.call-update
  116.3 0.0 copy-done.7
  116.3 0.1 power_multiply_fusion
  116.4 2.1 divide_select_fusion.k_ref
  118.6 0.0 copy-done.5
  118.6 4.7 %convolution_convert_fusion.x_ref = bf16[512,2048]{1,0:T(8,128)(2,1)S(1)} fusion(bf16[1024,512]{1,0:T(8,128)(2,1)S(1)} %copy-done.5, bf16[1024,2048]{1,0:T(8,128)(2,1)} %copy-done.1), kind=kOutput, calls=%fused_computation | convolution fusion | flops 2148532224 | bytes 7340032 | tf_op jit(solution)/shard_map/dot_general | solution.py:433
  123.3 3.7 %fusion.3 = f32[1024,512]{1,0:T(8,128)} fusion(bf16[1024,2048]{1,0:T(8,128)(2,1)S(1)} %copy-done.2, bf16[2048,512]{1,0:T(8,128)(2,1)S(1)} %copy-done), kind=kOutput, calls=%fused_computation.18 | convolution fusion | flops 2147483648 | bytes 8388608 | tf_op jit(solution)/shard_map/dot_general | solution.py:433
  127.0 137.2 %shard_map.57 = bf16[512,2048]{1,0:T(8,128)(2,1)S(1)} custom-call(bf16[512,2048]{1,0:T(8,128)(2,1)S(1)} %convolution_convert_fusion.x_ref, bf16[8,2048,256]{2,1,0:T(8,128)(2,1)} %get-tuple-element.12.v_ref, f32[256,2048]{1,0:T(8,128)} %divide_select_fusion.k_ref), custom_call_target="tpu_custom_call" | custom-call | flops 8000000000 | bytes 16777216 | tf_op jit(solution)/shard_map/pallas_call | solution.py:108
  264.2 1.3 copy-done.3
  265.5 6.8 %add_convert_fusion = bf16[1024,512]{1,0:T(8,128)(2,1)} fusion(f32[1024,512]{1,0:T(8,128)} %fusion.3, bf16[1024,2048]{1,0:T(8,128)(2,1)} %all-gather.2.cloned.1.call-done, bf16[512,2048]{1,0:T(8,128)(2,1)} %copy-done.3), kind=kOutput, calls=%fused_computation.7 | convolution fusion | flops 2148532224 | bytes 9437184 | tf_op jit(solution)/shard_map/dot_general | solution.py:433
  (15 shorter events, 0.1 us)
Async XLA Ops:
  6.5 116.8 %copy-start = (bf16[2048,512]{1,0:T(8,128)(2,1)S(1)}, bf16[2048,512]{1,0:T(8,128)(2,1)}, u32[]{:S(2)}) copy-start(bf16[2048,512]{1,0:T(8,128)(2,1)} %param.9) | copy-start | bytes 6291460
  6.5 259.0 %all-gather.2.cloned.1.call-start = ((), (), s32[]{:S(2)}) async-start(), calls=%async_computation | async-start | bytes 5242880 | tf_op jit(solution)/shard_map/all_gather | solution.py:474
  16.0 1.6 copy-start.6
  16.1 1.7 copy-start.4
  18.9 97.4 %copy-start.7 = (f32[2048]{0:T(1024)S(1)}, f32[2048]{0:T(1024)}, u32[]{:S(2)}) copy-start(f32[2048]{0:T(1024)} %param.8) | copy-start | bytes 24580
  114.3 1.9 copy-start.1
  116.3 2.3 copy-start.5
  118.6 4.7 %copy-start.2 = (bf16[1024,2048]{1,0:T(8,128)(2,1)S(1)}, bf16[1024,2048]{1,0:T(8,128)(2,1)}, u32[]{:S(2)}) copy-start(bf16[1024,2048]{1,0:T(8,128)(2,1)} %copy-done.1) | copy-start | bytes 12582916
  264.2 1.3 copy-start.3
Sparse Core Ops, SparseCore 0:
  116.4 99.9 all-gather.1

commit v4 on v3

--- a/solution.py
+++ b/solution.py
@@ -141,8 +141,8 @@
     return pl.ds(pl.multiple_of(index * width, width), width)
 
 
-def chain_kernel(n, zn, scale, x_ref, v_ref, k_ref, o_ref, landed, stage, parts, c_col, turned, rows,
-                 t_out, t_in, spread, n_out, n_in, own_q, rs, zs, ss, ts, ns, gs):
+def chain_kernel(n, zn, chunks, scale, x_ref, v_ref, k_ref, f_ref, o_ref, f_out, landed, stage, parts, c_col, turned, rows,
+                 t_out, t_in, spread, n_out, n_in, own_q, rs, zs, ss, ts, ns, gs, fs):
     me, z = lax.axis_index("rows"), lax.axis_index("feat")
     core, chip = lax.rem(me, 2), me // 2
     mate = me + 1 - 2 * core
@@ -155,6 +155,38 @@
     for d in range(1, zn):
         pl.semaphore_signal(barrier, inc=1, device_id={"feat": lax.rem(z + d, zn)}, device_id_type=MESH)
     pl.semaphore_wait(barrier, n + zn - 2)
+    ck = f_ref.shape[0] // chunks
+
+    def hop(way, step, unit):
+        there = f_out.at[pl.ds(unit * ck, ck), lanes(z - step if way == 0 else z + step, own)]
+        src = there if step else f_ref.at[pl.ds(unit * ck, ck)]
+        target = lax.rem(z + (1 if way == 0 else zn - 1), zn)
+        return remote(src, there, fs[0].at[way, step, unit], fs[1].at[way, step, unit], "feat", target)
+
+    def held(way, step):
+        return z >= step if way == 0 else z + step < zn
+
+    def onward(way):
+        return z < zn - 1 if way == 0 else z > 0
+
+    def forward(step, some):
+        for unit in some:
+            for way in (0, 1):
+                @pl.when(held(way, step))
+                def _():
+                    hop(way, step - 1, unit).wait_recv()
+                    if step < zn - 1:
+                        @pl.when(onward(way))
+                        def _():
+                            hop(way, step, unit).start()
+
+    every = range(chunks)
+    for unit in every:
+        for way in (0, 1):
+            @pl.when(onward(way))
+            def _():
+                hop(way, 0, unit).start()
+    f_out[:, lanes(z, own)] = f_ref[...]
 
     pending = []
     core_copies = []
@@ -203,6 +235,7 @@
         z_copies[d - 1].wait_recv()
         pass_tiles(lax.rem(z + zn - d, zn))
     pending += z_copies
+    forward(1, every)
 
     def add_rows(source):
         inner = c_col[source // per, pl.ds(pl.multiple_of(lax.rem(source, per) * nar, nar), nar)]
@@ -231,6 +264,9 @@
                 ins[me] = piece
         return copies
 
+    half = zn // 2
+    for step in range(2, half):
+        forward(step, every)
     t_copies = swap(lambda s: jnp.dot(rows[...], v_ref[s], preferred_element_type=f32), t_out, t_in, ts)
     for d in range(n):
         source = lax.rem(me + n - d, n)
@@ -238,6 +274,8 @@
             t_copies[d - 1].wait_recv()
         spread[:, lanes(source, nar)] = t_in[source].astype(f32).T.astype(bf16)
     pending += t_copies
+    if half > 1:
+        forward(half, every[: chunks // 2])
     for q in range(n):
         block = jnp.dot(spread[...], v_ref[q], preferred_element_type=f32)
         rows[:, pl.ds(q * nar, nar)] = (k_ref[:, pl.ds(q * nar, nar)] * block).astype(bf16)
@@ -254,6 +292,8 @@
 
     n_copies = swap(back, n_out, n_in, ns)
     pending += n_copies
+    if half > 1:
+        forward(half, every[chunks // 2 :])
     total = None
     for d in range(n):
         source = lax.rem(me + n - d, n)
@@ -279,13 +319,21 @@
         copy = remote(there, there, gs[2].at[d], gs[3].at[d], "rows", mate)
         copy.start()
         passed.append(copy)
+    for step in range(max(half, 1) + 1, zn):
+        forward(step, every)
     for copy in passed:
         copy.wait()
     for copy in copies + pending:
         copy.wait_send()
-
-
-def chain(part, v_pieces, kernel_rows, row_count):
+    for step in range(zn - 1):
+        for unit in every:
+            for way in (0, 1):
+                @pl.when(jnp.logical_and(held(way, step), onward(way)))
+                def _():
+                    hop(way, step, unit).wait_send()
+
+
+def chain(part, v_pieces, kernel_rows, x, row_count):
     n, zn = lax.axis_size("rows"), lax.axis_size("feat")
     own, d_all = part.shape
     nar, h = d_all // n, n // 2
@@ -296,9 +344,11 @@
     scratch += [pltpu.VMEM((nar, d_all), bf16), pltpu.VMEM(square, bf16), pltpu.VMEM(square, bf16)]
     scratch += [pltpu.VMEM((own, nar), bf16)]
     scratch += [[dma((h,))] * 4, [dma((zn - 1,))] * 2, [dma((n - 1,))] * 2, [dma((n - 1,))] * 2]
-    scratch += [[dma((n - 1,))] * 2, [dma((h,))] * 4]
-    kernel = functools.partial(chain_kernel, n, zn, 2.0 / row_count)
-    return call(kernel, jax.ShapeDtypeStruct((own, d_all), bf16), scratch, 9, 8 * part.nbytes, part, v_pieces, kernel_rows)
+    chunks = 4
+    scratch += [[dma((n - 1,))] * 2, [dma((h,))] * 4, [dma((2, zn - 1, chunks))] * 2]
+    kernel = functools.partial(chain_kernel, n, zn, chunks, 2.0 / row_count)
+    out = (jax.ShapeDtypeStruct((own, d_all), bf16), jax.ShapeDtypeStruct((x.shape[0], own * zn), bf16))
+    return call(kernel, out, scratch, 9, 8 * part.nbytes, part, v_pieces, kernel_rows, x)
 
 
 def front_kernel(n, zn, chunks, g_ref, v_ref, g_out, v_out, send, recv, near, far, mate_send, mate_recv):
@@ -470,12 +520,11 @@
     first = me * nar
     lam_row = lax.dynamic_slice_in_dim(eigvals, first, nar)
     kernel_rows = divided(lam_row, eigvals, first)
-    xc, g_all = lax.optimization_barrier((xc, g_all))
-    x_all = lax.all_gather(xc, "feat", axis=1, tiled=True)
     part = dot(xc, g_all, 0, 0).astype(bf16)
     if nar % 128 == 0:
-        sens = chain(part, v_pieces, kernel_rows, row_count)
+        sens, x_all = chain(part, v_pieces, kernel_rows, xc, row_count)
     else:
+        x_all = lax.all_gather(xc, "feat", axis=1, tiled=True)
         sens = chain_by_calls(part, v_pieces, kernel_rows, row_count)
     grad_in = dot(g_all, whiten, 1, 0) + dot(x_all, sens, 1, 1)
     return grad_in.astype(bf16)

time: 279 us -> 240 us (0.86)
  Pallas kernels: 239 us -> 220 us
  between operations: 13.5 us -> 0.15 us
    pallas_call x3, Pallas kernels: 239 us -> 220 us  [call(): pl.pallas_call(kernel, out_shape=out, in_specs=[VMEM] * len(args), out_sp...]
  transfers between devices with their start and end apart: 1 -> 0, of which waited for: 0 -> 0; matrix products, arithmetic and copies ran while one was open for 4% -> 0% of each run, Pallas kernels for 49% -> 0%
where the time goes in v4:
time: 240 us
  Pallas kernels  220 us (92%)
  matrix products  12.9 us (5%)
  other arithmetic  5.66 us (2%)
    pallas_call x3, Pallas kernels, call(): pl.pallas_call(kernel, out_shape=out, in_specs=[VMEM] * len(args), out_sp...  220 us
    dot_general x3, matrix products, dot(): lax.dot_general(a, b, (((ca,), (cb,)), ((), ())), preferred_element_type=...  12.9 us

profile of v4, /device:TPU:25, one launch (start us, length us, event | category | flops | bytes accessed | tf_op | source)
XLA Modules:
  0.0 240.0 jit_solution(12494671279678389483)
XLA Ops:
  0.0 0.0 copy-start
  0.0 1.6 convert_reduce_fusion.1
  1.6 1.4 convert_reduce_fusion
  3.0 0.0 copy-start.2
  3.0 6.4 %shard_map.55 = f32[8,8,512]{2,1,0:T(8,128)S(1)} custom-call(f32[8,512]{1,0:T(8,128)S(1)} %select_maximum_fusion.x_ref), custom_call_target="tpu_custom_call" | custom-call | flops 8000000000 | bytes 16384 | tf_op jit(solution)/shard_map/pallas_call | solution.py:108
  9.5 0.0 copy-start.4
  9.6 0.0 copy-done.2
  9.6 0.2 fusion.g_ref
  9.8 0.8 copy-done.4
  10.6 95.4 %shard_map.56 = (bf16[1024,2048]{1,0:T(8,128)(2,1)S(1)}, bf16[8,2048,256]{2,1,0:T(8,128)(2,1)}) custom-call(bf16[1024,512]{1,0:T(8,128)(2,1)S(1)} %fusion.g_ref, bf16[512,256]{1,0:T(8,128)(2,1)S(1)} %convert_element_type.28.v_ref), custom_call_target="tpu_custom_call" | custom-call | flops 8000000000 | bytes 4194304 | tf_op jit(solution)/shard_map/pallas_call | solution.py:108
  106.0 0.0 copy-done
  106.0 0.0 copy-start.3
  106.1 3.7 %fusion.3 = f32[1024,512]{1,0:T(8,128)} fusion(bf16[1024,2048]{1,0:T(8,128)(2,1)S(1)} %get-tuple-element.9, bf16[2048,512]{1,0:T(8,128)(2,1)S(1)} %copy-done), kind=kOutput, calls=%fused_computation.18 | convolution fusion | flops 2147483648 | bytes 8388608 | tf_op jit(solution)/shard_map/dot_general | solution.py:483
  109.7 0.0 copy-done.3
  109.7 0.2 fusion.1.f_ref
  109.9 0.0 copy-start.5
  109.9 3.8 %convolution_convert_fusion.x_ref = bf16[512,2048]{1,0:T(8,128)(2,1)} fusion(bf16[1024,512]{1,0:T(8,128)(2,1)S(1)} %fusion.1.f_ref, bf16[1024,2048]{1,0:T(8,128)(2,1)S(1)} %get-tuple-element.9), kind=kOutput, calls=%fused_computation | convolution fusion | flops 2148532224 | bytes 7340032 | tf_op jit(solution)/shard_map/dot_general | solution.py:483
  113.7 0.0 copy-done.5
  113.7 0.1 power_multiply_fusion
  113.8 2.1 divide_select_fusion.k_ref
  115.9 0.0 copy-done.1
  115.9 118.6 %shard_map.57 = (bf16[512,2048]{1,0:T(8,128)(2,1)S(1)}, bf16[1024,2048]{1,0:T(8,128)(2,1)}) custom-call(bf16[512,2048]{1,0:T(8,128)(2,1)S(1)} %copy-done.1, bf16[8,2048,256]{2,1,0:T(8,128)(2,1)} %get-tuple-element.10.v_ref, f32[256,2048]{1,0:T(8,128)} %divide_select_fusion.k_ref, bf16[1024,512]{1,0:T(8,128)(2,1)S(1)} %fusion.1.f_ref), custom_call_target="tpu_custom_call" | custom-call | flops 8000000000 | bytes 16777216 | tf_op jit(solution)/shard_map/pallas_call | solution.py:108
  234.5 0.0 copy-done.6
  234.5 5.5 %add_convert_fusion = bf16[1024,512]{1,0:T(8,128)(2,1)} fusion(f32[1024,512]{1,0:T(8,128)S(1)} %copy-done.6, bf16[1024,2048]{1,0:T(8,128)(2,1)} %get-tuple-element.11, bf16[512,2048]{1,0:T(8,128)(2,1)S(1)} %get-tuple-element.12), kind=kOutput, calls=%fused_computation.7 | convolution fusion | flops 2148532224 | bytes 9437184 | tf_op jit(solution)/shard_map/dot_general | solution.py:483
  (10 shorter events, 0.1 us)
Async XLA Ops:
  0.0 106.0 %copy-start = (bf16[2048,512]{1,0:T(8,128)(2,1)S(1)}, bf16[2048,512]{1,0:T(8,128)(2,1)}, u32[]{:S(2)}) copy-start(bf16[2048,512]{1,0:T(8,128)(2,1)} %param.9) | copy-start | bytes 6291460
  3.0 6.5 %copy-start.2 = (bf16[1024,512]{1,0:T(8,128)(2,1)S(1)}, bf16[1024,512]{1,0:T(8,128)(2,1)}, u32[]{:S(2)}) copy-start(bf16[1024,512]{1,0:T(8,128)(2,1)} %param.6) | copy-start | bytes 3145732
  9.5 1.0 copy-start.4
  106.0 3.7 %copy-start.3 = (bf16[1024,512]{1,0:T(8,128)(2,1)S(1)}, bf16[1024,512]{1,0:T(8,128)(2,1)}, u32[]{:S(2)}) copy-start(bf16[1024,512]{1,0:T(8,128)(2,1)} %param.5) | copy-start | bytes 3145732
  109.9 3.8 %copy-start.5 = (f32[2048]{0:T(1024)S(1)}, f32[2048]{0:T(1024)}, u32[]{:S(2)}) copy-start(f32[2048]{0:T(1024)} %param.8) | copy-start | bytes 24580
  113.7 2.2 copy-start.1
  115.9 118.6 %copy-start.6 = (f32[1024,512]{1,0:T(8,128)S(1)}, f32[1024,512]{1,0:T(8,128)}, u32[]{:S(2)}) copy-start(f32[1024,512]{1,0:T(8,128)} %fusion.3) | copy-start | bytes 6291460

commit v5 on v4

--- a/solution.py
+++ b/solution.py
@@ -181,11 +181,15 @@
                             hop(way, step, unit).start()
 
     every = range(chunks)
-    for unit in every:
-        for way in (0, 1):
-            @pl.when(onward(way))
-            def _():
-                hop(way, 0, unit).start()
+
+    def begin(some):
+        for unit in some:
+            for way in (0, 1):
+                @pl.when(onward(way))
+                def _():
+                    hop(way, 0, unit).start()
+
+    begin(every[: chunks // 2])
     f_out[:, lanes(z, own)] = f_ref[...]
 
     pending = []
@@ -230,6 +234,7 @@
         copy = remote(c_col.at[z], c_col.at[z], zs[0].at[d - 1], zs[1].at[d - 1], "feat", lax.rem(z + d, zn))
         copy.start()
         z_copies.append(copy)
+    begin(every[chunks // 2 :])
     pass_tiles(z)
     for d in range(1, zn):
         z_copies[d - 1].wait_recv()

time: 240 us -> 231 us (0.963)
  Pallas kernels: 220 us -> 211 us
    pallas_call x3, Pallas kernels: 220 us -> 211 us  [call(): pl.pallas_call(kernel, out_shape=out, in_specs=[VMEM] * len(args), out_sp...]
where the time goes in v5:
time: 231 us
  Pallas kernels  211 us (91%)
  matrix products  12.9 us (6%)
  other arithmetic  5.66 us (2%)
    pallas_call x3, Pallas kernels, call(): pl.pallas_call(kernel, out_shape=out, in_specs=[VMEM] * len(args), out_sp...  211 us
    dot_general x3, matrix products, dot(): lax.dot_general(a, b, (((ca,), (cb,)), ((), ())), preferred_element_type=...  12.9 us

profile of v5, /device:TPU:25, one launch (start us, length us, event | category | flops | bytes accessed | tf_op | source)
XLA Modules:
  0.0 230.9 jit_solution(1994651311941965054)
XLA Ops:
  0.0 0.0 copy-start
  0.0 1.6 convert_reduce_fusion.1
  1.6 1.4 convert_reduce_fusion
  3.0 0.0 copy-start.2
  3.0 6.4 %shard_map.55 = f32[8,8,512]{2,1,0:T(8,128)S(1)} custom-call(f32[8,512]{1,0:T(8,128)S(1)} %select_maximum_fusion.x_ref), custom_call_target="tpu_custom_call" | custom-call | flops 8000000000 | bytes 16384 | tf_op jit(solution)/shard_map/pallas_call | solution.py:108
  9.5 0.0 copy-start.4
  9.6 0.0 copy-done.2
  9.6 0.2 fusion.g_ref
  9.8 0.8 copy-done.4
  10.6 95.4 %shard_map.56 = (bf16[1024,2048]{1,0:T(8,128)(2,1)S(1)}, bf16[8,2048,256]{2,1,0:T(8,128)(2,1)}) custom-call(bf16[1024,512]{1,0:T(8,128)(2,1)S(1)} %fusion.g_ref, bf16[512,256]{1,0:T(8,128)(2,1)S(1)} %convert_element_type.28.v_ref), custom_call_target="tpu_custom_call" | custom-call | flops 8000000000 | bytes 4194304 | tf_op jit(solution)/shard_map/pallas_call | solution.py:108
  106.0 0.0 copy-done
  106.0 0.0 copy-start.3
  106.1 3.7 %fusion.3 = f32[1024,512]{1,0:T(8,128)} fusion(bf16[1024,2048]{1,0:T(8,128)(2,1)S(1)} %get-tuple-element.9, bf16[2048,512]{1,0:T(8,128)(2,1)S(1)} %copy-done), kind=kOutput, calls=%fused_computation.18 | convolution fusion | flops 2147483648 | bytes 8388608 | tf_op jit(solution)/shard_map/dot_general | solution.py:488
  109.7 0.0 copy-done.3
  109.7 0.2 fusion.1.f_ref
  109.9 0.0 copy-start.5
  109.9 3.8 %convolution_convert_fusion.x_ref = bf16[512,2048]{1,0:T(8,128)(2,1)} fusion(bf16[1024,512]{1,0:T(8,128)(2,1)S(1)} %fusion.1.f_ref, bf16[1024,2048]{1,0:T(8,128)(2,1)S(1)} %get-tuple-element.9), kind=kOutput, calls=%fused_computation | convolution fusion | flops 2148532224 | bytes 7340032 | tf_op jit(solution)/shard_map/dot_general | solution.py:488
  113.7 0.0 copy-done.5
  113.7 0.1 power_multiply_fusion
  113.8 2.1 divide_select_fusion.k_ref
  115.9 0.0 copy-done.1
  115.9 109.4 %shard_map.57 = (bf16[512,2048]{1,0:T(8,128)(2,1)S(1)}, bf16[1024,2048]{1,0:T(8,128)(2,1)}) custom-call(bf16[512,2048]{1,0:T(8,128)(2,1)S(1)} %copy-done.1, bf16[8,2048,256]{2,1,0:T(8,128)(2,1)} %get-tuple-element.10.v_ref, f32[256,2048]{1,0:T(8,128)} %divide_select_fusion.k_ref, bf16[1024,512]{1,0:T(8,128)(2,1)S(1)} %fusion.1.f_ref), custom_call_target="tpu_custom_call" | custom-call | flops 8000000000 | bytes 16777216 | tf_op jit(solution)/shard_map/pallas_call | solution.py:108
  225.4 0.0 copy-done.6
  225.4 5.5 %add_convert_fusion = bf16[1024,512]{1,0:T(8,128)(2,1)} fusion(f32[1024,512]{1,0:T(8,128)S(1)} %copy-done.6, bf16[1024,2048]{1,0:T(8,128)(2,1)} %get-tuple-element.11, bf16[512,2048]{1,0:T(8,128)(2,1)S(1)} %get-tuple-element.12), kind=kOutput, calls=%fused_computation.7 | convolution fusion | flops 2148532224 | bytes 9437184 | tf_op jit(solution)/shard_map/dot_general | solution.py:488
  (10 shorter events, 0.1 us)
Async XLA Ops:
  0.0 106.0 %copy-start = (bf16[2048,512]{1,0:T(8,128)(2,1)S(1)}, bf16[2048,512]{1,0:T(8,128)(2,1)}, u32[]{:S(2)}) copy-start(bf16[2048,512]{1,0:T(8,128)(2,1)} %param.9) | copy-start | bytes 6291460
  3.0 6.5 %copy-start.2 = (bf16[1024,512]{1,0:T(8,128)(2,1)S(1)}, bf16[1024,512]{1,0:T(8,128)(2,1)}, u32[]{:S(2)}) copy-start(bf16[1024,512]{1,0:T(8,128)(2,1)} %param.6) | copy-start | bytes 3145732
  9.5 1.0 copy-start.4
  106.0 3.7 %copy-start.3 = (bf16[1024,512]{1,0:T(8,128)(2,1)S(1)}, bf16[1024,512]{1,0:T(8,128)(2,1)}, u32[]{:S(2)}) copy-start(bf16[1024,512]{1,0:T(8,128)(2,1)} %param.5) | copy-start | bytes 3145732
  109.9 3.8 %copy-start.5 = (f32[2048]{0:T(1024)S(1)}, f32[2048]{0:T(1024)}, u32[]{:S(2)}) copy-start(f32[2048]{0:T(1024)} %param.8) | copy-start | bytes 24580
  113.7 2.2 copy-start.1
  115.9 109.4 %copy-start.6 = (f32[1024,512]{1,0:T(8,128)S(1)}, f32[1024,512]{1,0:T(8,128)}, u32[]{:S(2)}) copy-start(f32[1024,512]{1,0:T(8,128)} %fusion.3) | copy-start | bytes 6291460
